TPU v7x, 32 devices: a whole 2x2x4 slice. The times are simulated.
32 devices in a mesh: rep: 2 (over y), exp: 4 (over x, core), tp: 4 (over z).
Axes of the slice: x: 2, y: 2, z: 4, core: 2. Of those that a mesh axis runs over, the one named last changes fastest.
Arguments:
- tokens: bfloat16 [256, 6144], P(('rep', 'exp'), 'tp'), parts along dimension 0, may hold values from -6 to 6
- expert_ids: int32 [256, 2], P(('rep', 'exp')), parts along dimension 0, may hold values from 0 to 3, all different within a row; in each aligned block of 32 rows (0 to 31, 32 to 63, ...) at most 20 rows name the same one
- route_logits: float32 [256, 2], P(('rep', 'exp')), parts along dimension 0, may hold values from -6 to 6
- gate_weight: bfloat16 [6144, 32768], P(None, ('exp', 'tp')), may hold values from -0.078125 to 0.078125
- up_weight: bfloat16 [6144, 32768], P(None, ('exp', 'tp')), may hold values from -0.078125 to 0.078125
- down_weight: bfloat16 [32768, 6144], P(('exp', 'tp')), may hold values from -0.0625 to 0.0625
Outputs:
- moe_out: bfloat16 [256, 6144], P(('rep', 'exp'), 'tp'), parts along dimension 0
There are 2 independent parts, one for each index of `rep`. A program takes and returns all parts, laid end to end along the dimension named above; an argument that names none is the same for every part. Nothing has to cross between parts.
Inputs may be any that keep to these rules, and one draw needn't show every extreme that they name: `expert_ids`: each token names two different experts. In each aligned block of 32 tokens no expert is named by more than 20 tokens, a bound that some block reaches.
All inputs are finite; a program needn't handle non-finite values.
Results may differ from a plain program's by a relative error of at most 0.019.
Values may be sent and summed in bfloat16 or wider, within the bound.
A program may use at most 128 MiB of HBM per device.

v0:
```python
import jax
import jax.numpy as jnp
from jax import lax
from jax.sharding import PartitionSpec as P

D = 6144
EXPERTS = 4
CAP = 20


def slot_tables(expert_ids, route_logits):
    chosen = (expert_ids[:, :, None] == jnp.arange(EXPERTS, dtype=jnp.int32)[None, None, :]).astype(
        jnp.int32
    )
    per_token = jnp.sum(chosen, axis=1)
    before = jnp.cumsum(per_token, axis=0) - per_token
    position = jnp.sum(chosen * before[:, None, :], axis=2)
    at_slot = (position[:, :, None] == jnp.arange(CAP, dtype=jnp.int32)[None, None, :]).astype(
        jnp.float32
    )
    chosen_f = chosen.astype(jnp.float32)
    diff = route_logits[:, 0] - route_logits[:, 1]
    shares = jnp.stack([jax.nn.sigmoid(diff), jax.nn.sigmoid(-diff)], axis=1)
    placement = jnp.einsum("tke,tkc->ect", chosen_f, at_slot)
    mixing = jnp.einsum("tk,tke,tkc->tec", shares, chosen_f, at_slot)
    return (placement.astype(jnp.bfloat16), mixing)


def on_device(tokens, expert_ids, route_logits, gate_weight, up_weight, down_weight):
    exp_count = lax.axis_size("exp")
    groups = exp_count // EXPERTS
    placement, mixing = slot_tables(expert_ids, route_logits)
    whole_rows = lax.all_gather(tokens, "tp", axis=1, tiled=True)
    slots = jnp.einsum(
        "ect,td->ecd", placement, whole_rows, preferred_element_type=jnp.float32
    ).astype(jnp.bfloat16)
    outgoing = jnp.repeat(slots, groups, axis=0)
    gathered = lax.all_to_all(outgoing, "exp", split_axis=0, concat_axis=0, tiled=True)
    slot_rows = gathered.reshape(exp_count * CAP, D)
    gate_act = jnp.dot(slot_rows, gate_weight, preferred_element_type=jnp.float32)
    up_act = jnp.dot(slot_rows, up_weight, preferred_element_type=jnp.float32)
    hidden = (jax.nn.silu(gate_act) * up_act).astype(jnp.bfloat16)
    partial_value = jnp.dot(hidden, down_weight, preferred_element_type=jnp.float32).astype(
        jnp.bfloat16
    )
    partial_value = lax.optimization_barrier(partial_value).reshape(exp_count, CAP, D)
    narrow = lax.psum_scatter(
        partial_value.astype(jnp.float32).astype(jnp.bfloat16),
        "tp",
        scatter_dimension=2,
        tiled=True,
    ).astype(jnp.float32)
    returned = lax.all_to_all(
        narrow.astype(jnp.bfloat16), "exp", split_axis=0, concat_axis=0, tiled=True
    ).astype(narrow.dtype)
    summed = jnp.sum(returned.reshape(EXPERTS, groups, CAP, returned.shape[2]), axis=1)
    moe_out = jnp.einsum("tec,ecd->td", mixing, summed, precision=lax.Precision.HIGHEST).astype(
        jnp.bfloat16
    )
    return moe_out


def solution(mesh):
    return jax.shard_map(
        on_device,
        mesh=mesh,
        in_specs=(
            P(("rep", "exp"), "tp"),
            P(("rep", "exp"), None),
            P(("rep", "exp"), None),
            P(None, ("exp", "tp")),
            P(None, ("exp", "tp")),
            P(("exp", "tp"), None),
        ),
        out_specs=P(("rep", "exp"), "tp"),
        check_vma=False,
    )
```

profile of v0, /device:TPU:0, one launch (start us, length us, event | category | flops | bytes accessed | tf_op | source)
XLA Modules:
  0.0 124.6 jit_solution(4549421285769029820)
XLA Ops:
  6.5 0.0 reduce-scatter.2.cloned.1.call-start
  6.5 0.7 convert_reduce_fusion
  7.2 0.7 convert_convert_fusion
  7.9 0.1 copy.11
  8.0 0.1 reduce_window_sum.11
  8.1 0.1 copy.13
  8.1 0.7 select_reduce_fusion
  8.8 0.1 copy.14
  8.9 0.1 copy.16
  9.0 16.5 %all_gather.3 = bf16[32,6144]{1,0:T(8,128)(2,1)S(1)} all-gather(bf16[32,1536]{1,0:T(8,128)(2,1)} %param.6), channel_id=1, replica_groups=mesh['rep'=2,'exp'=4,'tp'=4] {'tp'}, dimensions={1}, use_global_device_ids=true | all-gather | bytes 491520 | tf_op jit(solution)/shard_map/all_gather | solution.py:33
  25.5 0.3 fusion.2
  25.8 0.5 convolution_convert_fusion
  26.3 18.4 %all_to_all.10 = bf16[4,20,6144]{2,1,0:T(8,128)(2,1)S(1)} all-to-all(bf16[4,20,6144]{2,1,0:T(8,128)(2,1)S(1)} %convolution_convert_fusion), channel_id=1, replica_groups=mesh['rep'=2,'exp'=4,'tp'=4] {'exp'}, dimensions={0} | all-to-all | bytes 1966080 | tf_op jit(solution)/shard_map/all_to_all | solution.py:38
  44.7 0.3 reshape.20
  45.0 10.5 %fusion.16 = f32[80,2048]{1,0:T(8,128)S(1)} fusion(bf16[80,6144]{1,0:T(8,128)(2,1)S(1)} %reshape.20, bf16[6144,2048]{1,0:T(8,128)(2,1)} %param.9), kind=kOutput, calls=%fused_computation.31 | convolution fusion | flops 2013265920 | bytes 26804224 | tf_op jit(solution)/shard_map/dot_general | solution.py:40
  55.4 0.0 copy-start.1
  55.4 0.0 copy-start
  55.5 19.9 %convolution_convert_fusion.1 = bf16[80,6144]{1,0:T(8,128)(2,1)S(1)} fusion(bf16[2048,6144]{1,0:T(8,128)(2,1)} %param.11, bf16[80,6144]{1,0:T(8,128)(2,1)S(1)} %reshape.20, bf16[6144,2048]{1,0:T(8,128)(2,1)} %param.10, f32[80,2048]{1,0:T(8,128)S(1)} %fusion.16), kind=kOutput, calls=%fused_computation.1 | convolution fusion | flops 4028006400 | bytes 52953088 | tf_op jit(solution)/shard_map/dot_general | solution.py:43
  75.4 1.1 reshape.21
  76.5 0.0 reduce-scatter.2.cloned.1.call-update
  76.5 0.0 copy-done.1
  76.6 0.0 copy-done
  76.6 0.1 copy.15
  76.7 30.1 %reduce-scatter.2.cloned.1.call-done = bf16[4,20,1536]{2,1,0:T(8,128)(2,1)} async-done(((bf16[4,20,6144]{2,1,0:T(8,128)(2,1)}), bf16[4,20,1536]{2,1,0:T(8,128)(2,1)}) %reduce-scatter.2.cloned.1.call-update) | async-done | bytes 245776 | tf_op jit(solution)/shard_map/reduce_scatter | solution.py:47
  106.9 3.5 %all-to-all-start.1 = ((bf16[4,20,1536]{2,1,0:T(8,128)(2,1)}), bf16[4,20,1536]{2,1,0:T(8,128)(2,1)S(1)}, u32[]{:S(2)}, u32[]{:S(2)}) async-start(bf16[4,20,1536]{2,1,0:T(8,128)(2,1)} %reduce-scatter.2.cloned.1.call-done), calls=%async_computation.2 | async-start | bytes 589824 | tf_op jit(solution)/shard_map/all_to_all | solution.py:53
  110.3 0.3 fusion.12
  110.6 6.1 %all-to-all-done.1 = bf16[4,20,1536]{2,1,0:T(8,128)(2,1)S(1)} async-done(((bf16[4,20,1536]{2,1,0:T(8,128)(2,1)}), bf16[4,20,1536]{2,1,0:T(8,128)(2,1)S(1)}, u32[]{:S(2)}, u32[]{:S(2)}) %all-to-all-start.1) | async-done | bytes 245792 | tf_op jit(solution)/shard_map/all_to_all | solution.py:53
  116.6 1.1 fusion.1
  (4 shorter events, 0.0 us)
Async XLA Ops:
  6.5 100.3 %reduce-scatter.2.cloned.1.call-start = ((), (), s32[]{:S(2)}) async-start(), calls=%async_computation.3 | async-start | bytes 1474560 | tf_op jit(solution)/shard_map/reduce_scatter | solution.py:47
  55.4 21.1 %copy-start.1 = (f32[32,2]{0,1:T(2,128)S(1)}, f32[32,2]{0,1:T(2,128)}, u32[]{:S(2)}) copy-start(f32[32,2]{0,1:T(2,128)} %param.8) | copy-start | bytes 772
  55.4 21.1 %copy-start = (s32[32,2]{0,1:T(2,128)S(1)}, s32[32,2]{0,1:T(2,128)}, u32[]{:S(2)}) copy-start(s32[32,2]{0,1:T(2,128)} %param.7) | copy-start | bytes 772
  106.9 9.8 %all-to-all-start.1 = ((bf16[4,20,1536]{2,1,0:T(8,128)(2,1)}), bf16[4,20,1536]{2,1,0:T(8,128)(2,1)S(1)}, u32[]{:S(2)}, u32[]{:S(2)}) async-start(bf16[4,20,1536]{2,1,0:T(8,128)(2,1)} %reduce-scatter.2.cloned.1.call-done), calls=%async_computation.2 | async-start | bytes 589824 | tf_op jit(solution)/shard_map/all_to_all | solution.py:53
Sparse Core Ops, SparseCore 0:
  76.7 30.1 reduce-scatter.1
where the time goes:
time: 125 us
  waiting for transfers between devices  36.2 us (29%)
  blocking collectives  34.9 us (28%)
  matrix products  32.5 us (26%)
  between operations  13.5 us (11%)
  starting transfers between devices  3.45 us (3%)
  other arithmetic  2.17 us (2%)
  local copies, waits for them, and re-layouts  1.89 us (2%)
    reduce_scatter x1, waiting for transfers between devices, on_device(): lax.psum_scatter(partial_value.astype(jnp.float32).astype(jnp.bfloat16),...  30.1 us
    dot_general x1, matrix products, on_device(): jnp.dot(hidden, down_weight, preferred_element_type=jnp.float32)  19.9 us
    all_to_all x1, blocking collectives, on_device(): lax.all_to_all(outgoing, 'exp', split_axis=0, concat_axis=0, tiled=True)  18.4 us
    all_gather x1, blocking collectives, on_device(): whole_rows = lax.all_gather(tokens, 'tp', axis=1, tiled=True)  16.5 us
    dot_general x1, matrix products, on_device(): jnp.dot(slot_rows, gate_weight, preferred_element_type=jnp.float32)  10.5 us
    all_to_all x1, waiting for transfers between devices, on_device(): lax.all_to_all(narrow.astype(jnp.bfloat16), 'exp', split_axis=0, concat_a...  6.06 us
    all_to_all x1, starting transfers between devices, on_device(): lax.all_to_all(narrow.astype(jnp.bfloat16), 'exp', split_axis=0, concat_a...  3.45 us
  transfers between devices with their start and end apart: 2, of which 2 were waited for; matrix products, arithmetic and copies ran while one was open for 0% of the time, Pallas kernels for 0%

commit v1 on v0

--- a/solution.py
+++ b/solution.py
@@ -1,3 +1,4 @@
+import functools
 import jax
 import jax.numpy as jnp
 from jax import lax
@@ -6,6 +7,13 @@
 D = 6144
 EXPERTS = 4
 CAP = 20
+
+
+def routes_all_load(message, axis_tag):
+    return jnp.concatenate(lax.all_gather(message, axis_name=axis_tag), 1)
+
+
+unite_sheet_here = functools.partial(routes_all_load, axis_tag="tp")
 
 
 def slot_tables(expert_ids, route_logits):
@@ -30,7 +38,7 @@
     exp_count = lax.axis_size("exp")
     groups = exp_count // EXPERTS
     placement, mixing = slot_tables(expert_ids, route_logits)
-    whole_rows = lax.all_gather(tokens, "tp", axis=1, tiled=True)
+    whole_rows = unite_sheet_here(tokens)
     slots = jnp.einsum(
         "ect,td->ecd", placement, whole_rows, preferred_element_type=jnp.float32
     ).astype(jnp.bfloat16)

time: 125 us -> 125 us (level)
  no operation moved by 1% of the time
where the time goes in v1:
time: 125 us
  waiting for transfers between devices  36.2 us (29%)
  blocking collectives  34.9 us (28%)
  matrix products  32.5 us (26%)
  between operations  13.5 us (11%)
  starting transfers between devices  3.45 us (3%)
  local copies, waits for them, and re-layouts  2.48 us (2%)
  other arithmetic  2.17 us (2%)
    reduce_scatter x1, waiting for transfers between devices, on_device(): lax.psum_scatter(partial_value.astype(jnp.float32).astype(jnp.bfloat16),...  30.1 us
    dot_general x1, matrix products, on_device(): jnp.dot(hidden, down_weight, preferred_element_type=jnp.float32)  19.9 us
    all_to_all x1, blocking collectives, on_device(): lax.all_to_all(outgoing, 'exp', split_axis=0, concat_axis=0, tiled=True)  18.4 us
    all_gather x1, blocking collectives, routes_all_load(): return jnp.concatenate(lax.all_gather(message, axis_name=axis_tag), 1)  16.5 us
    dot_general x1, matrix products, on_device(): jnp.dot(slot_rows, gate_weight, preferred_element_type=jnp.float32)  10.5 us
    all_to_all x1, waiting for transfers between devices, on_device(): lax.all_to_all(narrow.astype(jnp.bfloat16), 'exp', split_axis=0, concat_a...  6.06 us
    all_to_all x1, starting transfers between devices, on_device(): lax.all_to_all(narrow.astype(jnp.bfloat16), 'exp', split_axis=0, concat_a...  3.45 us
  transfers between devices with their start and end apart: 2, of which 2 were waited for; matrix products, arithmetic and copies ran while one was open for 0% of the time, Pallas kernels for 0%

profile of v1, /device:TPU:0, one launch (start us, length us, event | category | flops | bytes accessed | tf_op | source)
XLA Modules:
  0.0 125.1 jit_solution(4094414334063270027)
XLA Ops:
  6.5 0.0 reduce-scatter.2.cloned.1.call-start
  6.5 0.7 convert_reduce_fusion
  7.2 0.7 convert_convert_fusion
  7.9 0.1 copy.13
  8.0 0.1 reduce_window_sum.11
  8.1 0.1 copy.15
  8.1 0.7 select_reduce_fusion
  8.8 0.1 copy.16
  8.9 0.1 copy.18
  9.0 16.5 %all-gather = bf16[128,1536]{1,0:T(8,128)(2,1)S(1)} all-gather(bf16[32,1536]{1,0:T(8,128)(2,1)} %param.6), channel_id=2, replica_groups=mesh['rep'=2,'exp'=4,'tp'=4] {'tp'}, dimensions={0}, use_global_device_ids=true | all-gather | bytes 491520 | tf_op jit(solution)/shard_map/all_gather | solution.py:13
  25.5 0.3 copy.27
  25.8 0.3 reshape.31
  26.1 0.3 fusion.2
  26.4 0.5 convolution_convert_fusion
  26.9 18.4 %all_to_all.10 = bf16[4,20,6144]{2,1,0:T(8,128)(2,1)S(1)} all-to-all(bf16[4,20,6144]{2,1,0:T(8,128)(2,1)S(1)} %convolution_convert_fusion), channel_id=1, replica_groups=mesh['rep'=2,'exp'=4,'tp'=4] {'exp'}, dimensions={0} | all-to-all | bytes 1966080 | tf_op jit(solution)/shard_map/all_to_all | solution.py:46
  45.3 0.3 reshape.28
  45.6 10.5 %fusion.15 = f32[80,2048]{1,0:T(8,128)S(1)} fusion(bf16[80,6144]{1,0:T(8,128)(2,1)S(1)} %reshape.28, bf16[6144,2048]{1,0:T(8,128)(2,1)} %param.9), kind=kOutput, calls=%fused_computation.31 | convolution fusion | flops 2013265920 | bytes 26804224 | tf_op jit(solution)/shard_map/dot_general | solution.py:48
  56.0 0.0 copy-start.1
  56.0 0.0 copy-start
  56.1 19.9 %convolution_convert_fusion.1 = bf16[80,6144]{1,0:T(8,128)(2,1)S(1)} fusion(bf16[2048,6144]{1,0:T(8,128)(2,1)} %param.11, bf16[80,6144]{1,0:T(8,128)(2,1)S(1)} %reshape.28, bf16[6144,2048]{1,0:T(8,128)(2,1)} %param.10, f32[80,2048]{1,0:T(8,128)S(1)} %fusion.15), kind=kOutput, calls=%fused_computation.1 | convolution fusion | flops 4028006400 | bytes 52953088 | tf_op jit(solution)/shard_map/dot_general | solution.py:51
  76.0 1.1 reshape.29
  77.1 0.0 reduce-scatter.2.cloned.1.call-update
  77.1 0.0 copy-done.1
  77.2 0.0 copy-done
  77.2 0.1 copy.17
  77.3 30.1 %reduce-scatter.2.cloned.1.call-done = bf16[4,20,1536]{2,1,0:T(8,128)(2,1)} async-done(((bf16[4,20,6144]{2,1,0:T(8,128)(2,1)}), bf16[4,20,1536]{2,1,0:T(8,128)(2,1)}) %reduce-scatter.2.cloned.1.call-update) | async-done | bytes 245776 | tf_op jit(solution)/shard_map/reduce_scatter | solution.py:55
  107.4 3.5 %all-to-all-start.1 = ((bf16[4,20,1536]{2,1,0:T(8,128)(2,1)}), bf16[4,20,1536]{2,1,0:T(8,128)(2,1)S(1)}, u32[]{:S(2)}, u32[]{:S(2)}) async-start(bf16[4,20,1536]{2,1,0:T(8,128)(2,1)} %reduce-scatter.2.cloned.1.call-done), calls=%async_computation.2 | async-start | bytes 589824 | tf_op jit(solution)/shard_map/all_to_all | solution.py:61
  110.9 0.3 fusion.11
  111.2 6.1 %all-to-all-done.1 = bf16[4,20,1536]{2,1,0:T(8,128)(2,1)S(1)} async-done(((bf16[4,20,1536]{2,1,0:T(8,128)(2,1)}), bf16[4,20,1536]{2,1,0:T(8,128)(2,1)S(1)}, u32[]{:S(2)}, u32[]{:S(2)}) %all-to-all-start.1) | async-done | bytes 245792 | tf_op jit(solution)/shard_map/all_to_all | solution.py:61
  117.2 1.1 fusion.1
  (4 shorter events, 0.0 us)
Async XLA Ops:
  6.5 100.9 %reduce-scatter.2.cloned.1.call-start = ((), (), s32[]{:S(2)}) async-start(), calls=%async_computation.3 | async-start | bytes 1474560 | tf_op jit(solution)/shard_map/reduce_scatter | solution.py:55
  56.0 21.1 %copy-start.1 = (f32[32,2]{0,1:T(2,128)S(1)}, f32[32,2]{0,1:T(2,128)}, u32[]{:S(2)}) copy-start(f32[32,2]{0,1:T(2,128)} %param.8) | copy-start | bytes 772
  56.0 21.1 %copy-start = (s32[32,2]{0,1:T(2,128)S(1)}, s32[32,2]{0,1:T(2,128)}, u32[]{:S(2)}) copy-start(s32[32,2]{0,1:T(2,128)} %param.7) | copy-start | bytes 772
  107.4 9.8 %all-to-all-start.1 = ((bf16[4,20,1536]{2,1,0:T(8,128)(2,1)}), bf16[4,20,1536]{2,1,0:T(8,128)(2,1)S(1)}, u32[]{:S(2)}, u32[]{:S(2)}) async-start(bf16[4,20,1536]{2,1,0:T(8,128)(2,1)} %reduce-scatter.2.cloned.1.call-done), calls=%async_computation.2 | async-start | bytes 589824 | tf_op jit(solution)/shard_map/all_to_all | solution.py:61
Sparse Core Ops, SparseCore 0:
  77.3 30.1 reduce-scatter.1
